TPU v7x, 32 devices: a whole 2x2x4 slice. The times are simulated.
32 devices in a mesh: cls: 4 (over y, x), org: 8 (over z, core).
Axes of the slice: x: 2, y: 2, z: 4, core: 2. Of those that a mesh axis runs over, the one named last changes fastest.
Arguments:
- flows_start: float32 [8, 49152], P('cls', 'org'), may hold values from 150 to 300
- interaction: float32 [8, 8, 49152], P('cls', None, 'org'), may hold values from 0.2 to 2
- free_time: float32 [8, 49152], P('cls', 'org'), may hold values from 0.01 to 0.1
- capacity: float32 [49152], P('org'), may hold values from 300 to 900
- demand: int32 [8, 8, 60], P('cls', 'org'), may hold values from 0 to 15
- incidence: int32 [2, 8, 8, 2, 49152], P(None, 'cls', 'org'), may hold values from 0 to 1073741823, as said below
- step_size: float32 [2], replicated, may hold values from 0.3 to 0.6
Outputs:
- flows: float32 [8, 49152], P('cls', 'org')
- costs: float32 [8, 49152], P('cls', 'org')
- skims: float32 [2, 8, 8, 60], P(None, 'cls', 'org')
- gaps: float32 [2], replicated
Inputs may be any that keep to these rules, and one draw needn't show every extreme that they name: Bit b of incidence[k, c, o, w, l] tells whether link l lies on class c's path from anchor o to destination w * 30 + b in iteration k; each path is the union of 4 runs of 64 consecutive links (counted cyclically over the links) at drawn starts, the first of which is shared by all 30 destinations of one word.
All inputs are finite; a program needn't handle non-finite values.
Results may differ from a plain program's by a relative error of at most 0.0013.
Values sent between devices are 32-bit elements; how exact they have to be, the bound alone decides.
A program may use at most 256 MiB of HBM per device.

v0:
```python
import jax
import jax.numpy as jnp
from jax import lax
from jax.sharding import PartitionSpec as P

BITS = 30
ITERS = 2
HIGH = lax.Precision.HIGHEST


def unpack_half(packed):
    shifts = jnp.arange(BITS, dtype=jnp.int32)
    bit_table = jnp.bitwise_and(jnp.right_shift(packed[..., :, None, :], shifts[:, None]), 1)
    new_shape = packed.shape[:-2] + (packed.shape[-2] * BITS, packed.shape[-1])
    return bit_table.reshape(new_shape).astype(jnp.bfloat16)


def link_cost(flows_all, inter, free, cap):
    load_sum = jnp.einsum("cel,el->cl", inter, flows_all, precision=HIGH)
    load_ratio = load_sum / cap
    square = load_ratio * load_ratio
    return free * (1.0 + 0.15 * square * square)


def split_three(values):
    upper = values.astype(jnp.bfloat16)
    remain = values - upper.astype(jnp.float32)
    middle = remain.astype(jnp.bfloat16)
    lowest = (remain - middle.astype(jnp.float32)).astype(jnp.bfloat16)
    return jnp.stack([upper, middle, lowest], axis=1)


def skim_block(bit_table, cost_block):
    parts = split_three(cost_block)
    terms = jnp.einsum("codl,cpl->cpod", bit_table, parts, preferred_element_type=jnp.float32)
    return jnp.sum(terms, axis=1)


def anchor_loads_local(packed_all, trips_half, link_shard, block_count):

    def one_block(block_index):
        word_block = lax.dynamic_slice_in_dim(packed_all, block_index * link_shard, link_shard, 3)
        bit_table = unpack_half(word_block)
        return jnp.einsum("cod,codl->cl", trips_half, bit_table, preferred_element_type=jnp.float32)

    blocks = lax.map(one_block, jnp.arange(block_count, dtype=jnp.int32))
    return jnp.moveaxis(blocks, 0, 1).reshape(blocks.shape[1], block_count * link_shard)


def make_fold(packed_all, link_shard):

    def fold_links(skim_carry, portion, first):
        turn_count = portion.shape[1] // link_shard

        def advance(skim_sum, block_index):
            offset = block_index * link_shard
            word_block = lax.dynamic_slice_in_dim(packed_all, offset, link_shard, 3)
            bit_table = unpack_half(word_block)
            cost_block = lax.dynamic_slice_in_dim(portion, offset, link_shard, 1)
            return (skim_sum + skim_block(bit_table, cost_block), None)

        result, unused = lax.scan(advance, skim_carry, jnp.arange(turn_count, dtype=jnp.int32))
        return result

    return fold_links


def both_totals(cost_part, path_part):
    return lax.psum((cost_part, path_part), ("cls", "org"))


def shards(flows_start, interaction, free_time, capacity, demand, incidence, step_size):
    org_count = lax.axis_size("org")
    link_shard = flows_start.shape[1]
    dest_count = demand.shape[2]
    class_local = demand.shape[0]
    demand_real = demand.astype(jnp.float32)
    trips_half = demand.astype(jnp.bfloat16)
    own_start = lax.axis_index("org") * link_shard
    skim_init = jnp.zeros((class_local, demand.shape[1], dest_count), jnp.float32)
    skim_list = []
    gap_list = []
    inter_full, free_full, cap_full, flow_now = (
        lax.all_gather(interaction, "org", axis=2, tiled=True),
        lax.all_gather(free_time, "org", axis=1, tiled=True),
        lax.all_gather(capacity, "org", axis=0, tiled=True),
        lax.all_gather(flows_start, "org", axis=1, tiled=True),
    )

    def full_cost(flow_value):
        flows_all = lax.all_gather(flow_value, "cls", axis=0, tiled=True)
        return link_cost(flows_all, inter_full, free_full, cap_full)

    for iteration in range(ITERS):
        cost_now = full_cost(flow_now)
        fold_links = make_fold(incidence[iteration], link_shard)
        skim_now = fold_links(skim_init, cost_now, jnp.int32(0))
        partial_value = anchor_loads_local(incidence[iteration], trips_half, link_shard, org_count)
        aon = lax.psum(partial_value, "org")
        product = lax.dynamic_slice_in_dim(cost_now * flow_now, own_start, link_shard, 1)
        cost_total, path_total = both_totals(jnp.sum(product), jnp.sum(demand_real * skim_now))
        gap_list.append((cost_total - path_total) / cost_total)
        skim_list.append(skim_now)
        flow_now = flow_now + step_size[iteration] * (aon - flow_now)
    cost_final = full_cost(flow_now)
    flow_out = lax.dynamic_slice_in_dim(flow_now, own_start, link_shard, 1)
    cost_out = lax.dynamic_slice_in_dim(cost_final, own_start, link_shard, 1)
    return (flow_out, cost_out, jnp.stack(skim_list), jnp.stack(gap_list))


def solution(mesh):
    placed = (
        P("cls", "org"),
        P("cls", None, "org"),
        P("cls", "org"),
        P("org"),
        P("cls", "org", None),
        P(None, "cls", "org", None, None),
        P(),
    )
    return jax.shard_map(
        shards,
        mesh=mesh,
        in_specs=placed,
        out_specs=(P("cls", "org"), P("cls", "org"), P(None, "cls", "org", None), P()),
        check_vma=False,
    )
```

profile of v0, /device:TPU:0, one launch (start us, length us, event | category | flops | bytes accessed | tf_op | source)
XLA Modules:
  0.0 387.4 jit_solution(10713880894416797273)
XLA Ops:
  10.9 32.3 %while.43 = (s32[]{:T(128)}, f32[8,2,6144]{2,1,0:T(2,128)S(1)}, s32[8]{0:T(128)S(1)}, s32[2,1,2,49152]{3,0,2,1:T(2,128)S(1)}, bf16[2,1,60]{2,0,1:T(2,128)(2,1)S(...) while((s32[]{:T(128)}, f32[8,2,6144]{2,1,0:T(2,128)S(1)}, s32[8]{0:T(128)S(1)}, ...), condition=%wide.region_4.5_spmd, body=%wide.region_3.4_spmd.sunk | while | flops 3686406 | bytes 3392847 | solution.py:46
  12.3 1.7 fusion.83
  16.3 1.7 fusion.83
  20.3 1.7 fusion.83
  24.4 1.7 fusion.83
  28.4 1.7 fusion.83
  32.5 1.7 fusion.83
  36.5 1.7 fusion.83
  40.5 1.7 fusion.83
  44.3 32.3 %while.42 = (s32[]{:T(128)}, f32[8,2,6144]{2,1,0:T(2,128)S(1)}, s32[8]{0:T(128)S(1)}, s32[2,1,2,49152]{3,0,2,1:T(2,128)S(1)}, bf16[2,1,60]{2,0,1:T(2,128)(2,1)S(...) while((s32[]{:T(128)}, f32[8,2,6144]{2,1,0:T(2,128)S(1)}, s32[8]{0:T(128)S(1)}, ...), condition=%wide.region_1.0_spmd, body=%wide.region_0.1_spmd.sunk | while | flops 3686406 | bytes 3392847 | solution.py:46
  45.7 1.7 fusion.79
  49.7 1.7 fusion.79
  53.8 1.7 fusion.79
  57.8 1.7 fusion.79
  61.8 1.7 fusion.79
  65.9 1.7 fusion.79
  69.9 1.7 fusion.79
  74.0 1.7 fusion.79
  77.5 17.5 %all_gather.21 = f32[2,49152]{1,0:T(2,128)} all-gather(f32[2,6144]{1,0:T(2,128)S(1)} %copy-done.7), channel_id=1, replica_groups=mesh['cls'=4,'org'=8] {'org'}, dimensions={1}, use_global_device_ids=true | all-gather | bytes 442368 | tf_op jit(solution)/shard_map/all_gather | solution.py:87
  95.7 42.7 %all-reduce.4.cloned.1.call-done = (f32[2,49152]{1,0:T(2,128)}, f32[2,49152]{1,0:T(2,128)}) async-done(((f32[2,49152]{1,0:T(2,128)}, f32[2,49152]{1,0:T(2,128)}), (f32[2,49152]{1,0:T(2,128)}, f32[2,49152]{1,0:T(2,128)})) %all-reduce.4.cloned.1.call-update) | async-done | bytes 786448 | tf_op jit(solution)/shard_map/psum | solution.py:99
  138.4 3.8 multiply_add_fusion
  143.5 15.2 %all_gather.25 = f32[49152]{0:T(1024)} all-gather(f32[6144]{0:T(1024)S(1)} %copy-done.9), channel_id=1, replica_groups=mesh['cls'=4,'org'=8] {'org'}, dimensions={0}, use_global_device_ids=true | all-gather | bytes 221184 | tf_op jit(solution)/shard_map/all_gather | solution.py:86
  158.7 14.7 %all_gather.22 = f32[2,49152]{1,0:T(2,128)S(1)} all-gather(f32[2,6144]{1,0:T(2,128)S(1)} %copy-done.8), channel_id=1, replica_groups=mesh['cls'=4,'org'=8] {'org'}, dimensions={1}, use_global_device_ids=true | all-gather | bytes 442368 | tf_op jit(solution)/shard_map/all_gather | solution.py:85
  174.8 2.5 reshape.94
  177.3 2.5 reshape.92
  179.8 24.8 %all-gather.14.cloned.1.call-done = f32[4,2,49152]{2,1,0:T(2,128)} async-done(((f32[1,2,49152]{2,1,0:T(2,128)}), f32[4,2,49152]{2,1,0:T(2,128)}) %all-gather.14.cloned.1.call-update) | async-done | bytes 1572880 | tf_op jit(solution)/shard_map/all_gather | solution.py:91
  204.6 3.6 reshape.96
  208.2 36.0 %all-gather.8.cloned.1.call-done = f32[2,8,49152]{2,1,0:T(8,128)} async-done(((f32[2,8,6144]{2,1,0:T(8,128)}), f32[2,8,49152]{2,1,0:T(8,128)}) %all-gather.8.cloned.1.call-update) | async-done | bytes 3145744 | tf_op jit(solution)/shard_map/all_gather | solution.py:84
  244.2 6.9 %multiply_reduce_fusion.1 = (f32[49152,2]{0,1:T(2,128)S(1)}, f32[49152,2]{0,1:T(2,128)S(1)}, f32[49152,2]{0,1:T(2,128)}) fusion(f32[2,8,49152]{2,1,0:T(8,128)} %all-gather.8.cloned.1.call-done, f32[49152,8]{0,1:T(8,128)S(1)} %bitcast.155, f32[49152,8]{0,1:T(8,128)} %bitcast.157, f32[49152,8]{0,1:T(8,128)S(1)} %bitcast.156), kind=kLoop, calls=%fused_computation.59 | loop fusion | flops 4423680 | bytes 9043968 | tf_op jit(solution)/shard_map/cel,el->cl/dot_general | solution.py:19
  253.4 39.4 %while.44 = (s32[]{:T(128)}, f32[2,1,60]{2,0,1:T(2,128)S(1)}, s32[8]{0:T(128)S(1)}, f32[2,49152]{1,0:T(2,128)S(1)}, s32[2,1,2,49152]{3,0,2,1:T(2,128)}, /*index=5*/s32[]{:T(128)}, s32[1]{0:T(128)}, s32[]{:T(128)}, s32[]{:T(128)}) while((s32[]{:T(128)}, f32[2,1,60]{2,0,1:T(2,128)S(1)}, s32[8]{0:T(128)S(1)}, ...), condition=%wide.region_8.9_spmd.clone, body=%wide.region_6.8_spmd.clone.sunk | while | flops 6943207 | bytes 3615725 | solution.py:62
  294.2 39.4 %while.45 = (s32[]{:T(128)}, f32[2,1,60]{2,0,1:T(2,128)S(1)}, s32[8]{0:T(128)S(1)}, f32[2,49152]{1,0:T(2,128)S(1)}, s32[2,1,2,49152]{3,0,2,1:T(2,128)}, /*index=5*/s32[]{:T(128)}, s32[1]{0:T(128)}, s32[]{:T(128)}, s32[]{:T(128)}) while((s32[]{:T(128)}, f32[2,1,60]{2,0,1:T(2,128)S(1)}, s32[8]{0:T(128)S(1)}, ...), condition=%wide.region_11.12_spmd.clone, body=%wide.region_9.11_spmd.clone.sunk | while | flops 6943207 | bytes 3615725 | solution.py:62
  334.2 39.7 %all-reduce = (f32[]{:T(128)}, f32[]{:T(128)}, f32[]{:T(128)}, f32[]{:T(128)}) all-reduce(f32[]{:T(128)} %fusion.53, f32[]{:T(128)} %get-tuple-element.186, f32[]{:T(128)} %fusion.54, f32[]{:T(128)} %get-tuple-element.185), channel_id=1, replica_groups=mesh['cls'=4,'org'=8] {'cls','org'}, use_global_device_ids=true, to_apply=%region_17.18 | all-reduce | flops 4 | bytes 32 | tf_op jit(solution)/shard_map/psum | solution.py:69
  (345 shorter events, 107.4 us)
Async XLA Ops:
  8.0 130.4 %all-reduce.4.cloned.1.call-start = ((), (), s32[]{:S(2)}) async-start(), calls=%async_computation.4 | async-start | bytes 1572864 | tf_op jit(solution)/shard_map/psum | solution.py:99
  8.0 1.5 copy-start.11
  43.2 1.0 copy-start
  43.2 1.1 copy-start.6
  43.3 34.1 %copy-start.7 = (f32[2,6144]{1,0:T(2,128)S(1)}, f32[2,6144]{1,0:T(2,128)}, u32[]{:S(2)}) copy-start(f32[2,6144]{1,0:T(2,128)} %param.15) | copy-start | bytes 147460
  76.6 0.8 copy-start.5
  76.6 65.5 %copy-start.1 = (s32[2,1,2,49152]{3,0,2,1:T(2,128)}, s32[2,1,2,49152]{3,0,2,1:T(2,128)S(1)}, u32[]{:S(2)}) copy-start(s32[2,1,2,49152]{3,0,2,1:T(2,128)S(1)} %get-tuple-element.496) | copy-start | bytes 2359300
  76.6 18.4 %copy-start.10 = (f32[2]{0:T(128)S(1)}, f32[2]{0:T(128)}, u32[]{:S(2)}) copy-start(f32[2]{0:T(128)} %param.21) | copy-start | bytes 28
  77.4 97.4 %all-gather.12.cloned.1.call-start = ((), (), s32[]{:S(2)}) async-start(), calls=%async_computation.2 | async-start | bytes 1966080 | tf_op jit(solution)/shard_map/all_gather | solution.py:91
  95.0 82.3 %all-gather.10.cloned.1.call-start = ((), (), s32[]{:S(2)}) async-start(), calls=%async_computation.1 | async-start | bytes 1966080 | tf_op jit(solution)/shard_map/all_gather | solution.py:91
  138.4 5.1 %copy-start.9 = (f32[6144]{0:T(1024)S(1)}, f32[6144]{0:T(1024)}, u32[]{:S(2)}) copy-start(f32[6144]{0:T(1024)} %param.18) | copy-start | bytes 73732
  138.4 20.3 %copy-start.8 = (f32[2,6144]{1,0:T(2,128)S(1)}, f32[2,6144]{1,0:T(2,128)}, u32[]{:S(2)}) copy-start(f32[2,6144]{1,0:T(2,128)} %param.17) | copy-start | bytes 147460
  142.2 62.4 %all-gather.14.cloned.1.call-start = ((), (), s32[]{:S(2)}) async-start(), calls=%async_computation.3 | async-start | bytes 1966080 | tf_op jit(solution)/shard_map/all_gather | solution.py:91
  142.8 101.5 %all-gather.8.cloned.1.call-start = ((), (), s32[]{:S(2)}) async-start(), calls=%async_computation | async-start | bytes 3538944 | tf_op jit(solution)/shard_map/all_gather | solution.py:84
  244.2 6.9 %copy-start.2 = (f32[49152]{0:T(1024)S(1)}, f32[49152]{0:T(1024)}, u32[]{:S(2)}) copy-start(f32[49152]{0:T(1024)} %all_gather.25) | copy-start | bytes 589828
  294.2 83.5 %copy-start.3 = (f32[49152]{0:T(1024)S(1)}, f32[49152]{0:T(1024)}, u32[]{:S(2)}) copy-start(f32[49152]{0:T(1024)} %all_gather.25) | copy-start | bytes 589828
  294.2 83.5 %copy-start.4 = (f32[49152,2]{0,1:T(2,128)S(1)}, f32[49152,2]{0,1:T(2,128)}, u32[]{:S(2)}) copy-start(f32[49152,2]{0,1:T(2,128)} %get-tuple-element.184) | copy-start | bytes 1179652
Sparse Core Ops, SparseCore 0:
  77.5 60.7 all-reduce.3
Sparse Core Ops, SparseCore 1:
  95.1 31.7 all-gather.11
  142.3 29.8 all-gather.9
  173.8 30.7 all-gather.13
  206.2 38.0 all-gather.7
where the time goes:
time: 389 us; the launch traced here: 387 us
  waiting for transfers between devices  105 us (27%)
  blocking collectives  87 us (22%)
  other arithmetic  73.1 us (19%)
  local copies, waits for them, and re-layouts  54.4 us (14%)
  matrix products  25.3 us (7%)
  loops' own time  22.7 us (6%)
  between operations  19.7 us (5%)
    convert_element_type x32, other arithmetic, unpack_half(): return bit_table.reshape(new_shape).astype(jnp.bfloat16)  55.2 us
    psum x1, waiting for transfers between devices, shards(): aon = lax.psum(partial_value, 'org')  42.7 us
    psum x1, blocking collectives, both_totals(): return lax.psum((cost_part, path_part), ('cls', 'org'))  39.7 us
    all_gather x1, waiting for transfers between devices, shards(): lax.all_gather(interaction, 'org', axis=2, tiled=True)  36 us
    all_gather x3, waiting for transfers between devices, full_cost(): flows_all = lax.all_gather(flow_value, 'cls', axis=0, tiled=True)  24.8 us
    dynamic_slice x32, local copies, waits for them, and re-layouts, fold_links(): lax.scan(advance, skim_carry, jnp.arange(turn_count, dtype=jnp.int32))  18.8 us
    all_gather x1, blocking collectives, shards(): lax.all_gather(flows_start, 'org', axis=1, tiled=True)  17.5 us
    shift_right_arithmetic x96, local copies, waits for them, and re-layouts, unpack_half(): jnp.right_shift(packed[..., :, None, :], shifts[:, None])  17.5 us
  transfers between devices with their start and end apart: 5, of which 3 were waited for; matrix products, arithmetic and copies ran while one was open for 4% of the time, Pallas kernels for 0%

commit v1 on v0

--- a/solution.py
+++ b/solution.py
@@ -2,10 +2,21 @@
 import jax.numpy as jnp
 from jax import lax
 from jax.sharding import PartitionSpec as P
+from jax.lax import ppermute, psum
 
 BITS = 30
 ITERS = 2
 HIGH = lax.Precision.HIGHEST
+
+
+def serve_fields(obj, bus_axis="org"):
+    axis_n = psum(1, bus_axis)
+    e_next = obj
+    main = lambda raw_out: [(kk, kk ^ raw_out) for kk in range(axis_n)]
+    for d in range(axis_n.bit_length() - 1):
+        s_next = main(1 << d)
+        e_next = e_next + ppermute(e_next, bus_axis, s_next)
+    return e_next
 
 
 def unpack_half(packed):
@@ -96,7 +107,7 @@
         fold_links = make_fold(incidence[iteration], link_shard)
         skim_now = fold_links(skim_init, cost_now, jnp.int32(0))
         partial_value = anchor_loads_local(incidence[iteration], trips_half, link_shard, org_count)
-        aon = lax.psum(partial_value, "org")
+        aon = serve_fields(partial_value)
         product = lax.dynamic_slice_in_dim(cost_now * flow_now, own_start, link_shard, 1)
         cost_total, path_total = both_totals(jnp.sum(product), jnp.sum(demand_real * skim_now))
         gap_list.append((cost_total - path_total) / cost_total)

time: 389 us -> 415 us (1.067)
  blocking collectives: 87 us -> 102 us
  starting transfers between devices: 0.21 us -> 8.56 us
  waiting for transfers between devices: 105 us -> 110 us
    psum x1 -> x0, waiting for transfers between devices: 42.7 us -> none  [shards(): aon = lax.psum(partial_value, 'org')]
    all_gather x3, waiting for transfers between devices: 24.8 us -> 52.7 us  [full_cost(): flows_all = lax.all_gather(flow_value, 'cls', axis=0, tiled=True)]
    ppermute x0 -> x6, waiting for transfers between devices: none -> 20.2 us  [serve_fields(): e_next = e_next + ppermute(e_next, bus_axis, s_next)]
    all_gather x1, blocking collectives: 17.5 us -> 32.9 us  [shards(): lax.all_gather(flows_start, 'org', axis=1, tiled=True)]
    ppermute x0 -> x6, starting transfers between devices: none -> 8.4 us  [serve_fields(): e_next = e_next + ppermute(e_next, bus_axis, s_next)]
    unnamed x27 -> x23, local copies, waits for them, and re-layouts: 10.4 us -> 9.03 us
  transfers between devices with their start and end apart: 5 -> 10, of which waited for: 3 -> 5; matrix products, arithmetic and copies ran while one was open for 4% -> 10% of each run, Pallas kernels for 0% -> 0%
where the time goes in v1:
time: 415 us; the launch traced here: 414 us
  waiting for transfers between devices  110 us (27%)
  blocking collectives  102 us (25%)
  other arithmetic  73.9 us (18%)
  local copies, waits for them, and re-layouts  53.1 us (13%)
  matrix products  25.3 us (6%)
  loops' own time  22.7 us (5%)
  between operations  17.9 us (4%)
  starting transfers between devices  8.56 us (2%)
    convert_element_type x32, other arithmetic, unpack_half(): return bit_table.reshape(new_shape).astype(jnp.bfloat16)  55.2 us
    all_gather x3, waiting for transfers between devices, full_cost(): flows_all = lax.all_gather(flow_value, 'cls', axis=0, tiled=True)  52.7 us
    psum x1, blocking collectives, both_totals(): return lax.psum((cost_part, path_part), ('cls', 'org'))  39.6 us
    all_gather x1, waiting for transfers between devices, shards(): lax.all_gather(interaction, 'org', axis=2, tiled=True)  36.1 us
    all_gather x1, blocking collectives, shards(): lax.all_gather(flows_start, 'org', axis=1, tiled=True)  32.9 us
    ppermute x6, waiting for transfers between devices, serve_fields(): e_next = e_next + ppermute(e_next, bus_axis, s_next)  20.2 us
    dynamic_slice x32, local copies, waits for them, and re-layouts, fold_links(): lax.scan(advance, skim_carry, jnp.arange(turn_count, dtype=jnp.int32))  18.8 us
    shift_right_arithmetic x96, local copies, waits for them, and re-layouts, unpack_half(): jnp.right_shift(packed[..., :, None, :], shifts[:, None])  17.5 us
  transfers between devices with their start and end apart: 10, of which 5 were waited for; matrix products, arithmetic and copies ran while one was open for 10% of the time, Pallas kernels for 0%

profile of v1, /device:TPU:0, one launch (start us, length us, event | category | flops | bytes accessed | tf_op | source)
XLA Modules:
  0.0 414.0 jit_solution(5425501579139453971)
XLA Ops:
  10.1 32.3 %while.42 = (s32[]{:T(128)}, f32[8,2,6144]{2,1,0:T(2,128)S(1)}, s32[8]{0:T(128)S(1)}, s32[2,1,2,49152]{3,0,2,1:T(2,128)S(1)}, bf16[2,1,60]{2,0,1:T(2,128)(2,1)S(...) while((s32[]{:T(128)}, f32[8,2,6144]{2,1,0:T(2,128)S(1)}, s32[8]{0:T(128)S(1)}, ...), condition=%wide.region_1.0_spmd, body=%wide.region_0.1_spmd.sunk | while | flops 3686406 | bytes 3392847 | solution.py:57
  11.4 1.7 fusion.79
  15.5 1.7 fusion.79
  19.5 1.7 fusion.79
  23.6 1.7 fusion.79
  27.6 1.7 fusion.79
  31.6 1.7 fusion.79
  35.7 1.7 fusion.79
  43.4 32.3 %while.43 = (s32[]{:T(128)}, f32[8,2,6144]{2,1,0:T(2,128)S(1)}, s32[8]{0:T(128)S(1)}, s32[2,1,2,49152]{3,0,2,1:T(2,128)S(1)}, bf16[2,1,60]{2,0,1:T(2,128)(2,1)S(...) while((s32[]{:T(128)}, f32[8,2,6144]{2,1,0:T(2,128)S(1)}, s32[8]{0:T(128)S(1)}, ...), condition=%wide.region_3.4_spmd, body=%wide.region_2.3_spmd.sunk | while | flops 3686406 | bytes 3392847 | solution.py:57
  48.7 1.7 fusion.83
  52.8 1.7 fusion.83
  56.8 1.7 fusion.83
  60.9 1.7 fusion.83
  64.9 1.7 fusion.83
  76.4 2.7 collective-permute-start.1
  80.8 8.3 %collective-permute-done.1 = f32[2,49152]{1,0:T(2,128)S(1)} collective-permute-done((f32[2,49152]{1,0:T(2,128)S(1)}, f32[2,49152]{1,0:T(2,128)S(1)}, u32[]{:S(2)}, u32[]{:S(2)}) %collective-permute-start.1) | collective-permute-done | bytes 393248 | tf_op jit(solution)/shard_map/ppermute | solution.py:18
  89.3 3.1 collective-permute-start.2
  92.4 11.9 %collective-permute-done.4 = f32[2,49152]{1,0:T(2,128)S(1)} collective-permute-done((f32[2,49152]{1,0:T(2,128)S(1)}, f32[2,49152]{1,0:T(2,128)S(1)}, u32[]{:S(2)}, u32[]{:S(2)}) %collective-permute-start.4) | collective-permute-done | bytes 393248 | tf_op jit(solution)/shard_map/ppermute | solution.py:18
  104.6 32.9 %all_gather.21 = f32[2,49152]{1,0:T(2,128)} all-gather(f32[2,6144]{1,0:T(2,128)S(1)} %copy-done.5), channel_id=1, replica_groups=mesh['cls'=4,'org'=8] {'org'}, dimensions={1}, use_global_device_ids=true | all-gather | bytes 442368 | tf_op jit(solution)/shard_map/all_gather | solution.py:98
  138.2 3.7 multiply_add_fusion
  143.3 15.2 %all_gather.25 = f32[49152]{0:T(1024)} all-gather(f32[6144]{0:T(1024)S(1)} %copy-done.7), channel_id=1, replica_groups=mesh['cls'=4,'org'=8] {'org'}, dimensions={0}, use_global_device_ids=true | all-gather | bytes 221184 | tf_op jit(solution)/shard_map/all_gather | solution.py:97
  158.4 14.6 %all_gather.22 = f32[2,49152]{1,0:T(2,128)S(1)} all-gather(f32[2,6144]{1,0:T(2,128)S(1)} %copy-done.6), channel_id=1, replica_groups=mesh['cls'=4,'org'=8] {'org'}, dimensions={1}, use_global_device_ids=true | all-gather | bytes 442368 | tf_op jit(solution)/shard_map/all_gather | solution.py:96
  174.5 2.6 reshape.94
  177.0 22.5 %all-gather.10.cloned.1.call-done = f32[4,2,49152]{2,1,0:T(2,128)} async-done(((f32[1,2,49152]{2,1,0:T(2,128)}), f32[4,2,49152]{2,1,0:T(2,128)}) %all-gather.10.cloned.1.call-update) | async-done | bytes 1572880 | tf_op jit(solution)/shard_map/all_gather | solution.py:102
  199.5 2.5 reshape.92
  202.0 30.2 %all-gather.14.cloned.1.call-done = f32[4,2,49152]{2,1,0:T(2,128)} async-done(((f32[1,2,49152]{2,1,0:T(2,128)}), f32[4,2,49152]{2,1,0:T(2,128)}) %all-gather.14.cloned.1.call-update) | async-done | bytes 1572880 | tf_op jit(solution)/shard_map/all_gather | solution.py:102
  232.2 3.6 reshape.96
  235.9 36.1 %all-gather.8.cloned.1.call-done = f32[2,8,49152]{2,1,0:T(8,128)} async-done(((f32[2,8,6144]{2,1,0:T(8,128)}), f32[2,8,49152]{2,1,0:T(8,128)}) %all-gather.8.cloned.1.call-update) | async-done | bytes 3145744 | tf_op jit(solution)/shard_map/all_gather | solution.py:95
  271.9 6.9 %multiply_reduce_fusion.1 = (f32[49152,2]{0,1:T(2,128)S(1)}, f32[49152,2]{0,1:T(2,128)S(1)}, f32[49152,2]{0,1:T(2,128)}) fusion(f32[2,8,49152]{2,1,0:T(8,128)} %all-gather.8.cloned.1.call-done, f32[49152,8]{0,1:T(8,128)S(1)} %bitcast.155, f32[49152,8]{0,1:T(8,128)} %bitcast.157, f32[49152,8]{0,1:T(8,128)S(1)} %bitcast.156), kind=kLoop, calls=%fused_computation.59 | loop fusion | flops 4423680 | bytes 9043968 | tf_op jit(solution)/shard_map/cel,el->cl/dot_general | solution.py:30
  281.1 39.4 %while.44 = (s32[]{:T(128)}, f32[2,1,60]{2,0,1:T(2,128)S(1)}, s32[8]{0:T(128)S(1)}, f32[2,49152]{1,0:T(2,128)S(1)}, s32[2,1,2,49152]{3,0,2,1:T(2,128)}, /*index=5*/s32[]{:T(128)}, s32[1]{0:T(128)}, s32[]{:T(128)}, s32[]{:T(128)}) while((s32[]{:T(128)}, f32[2,1,60]{2,0,1:T(2,128)S(1)}, s32[8]{0:T(128)S(1)}, ...), condition=%wide.region_6.7_spmd.clone, body=%wide.region_4.6_spmd.clone.sunk | while | flops 6943207 | bytes 3615725 | solution.py:73
  321.9 39.4 %while.45 = (s32[]{:T(128)}, f32[2,1,60]{2,0,1:T(2,128)S(1)}, s32[8]{0:T(128)S(1)}, f32[2,49152]{1,0:T(2,128)S(1)}, s32[2,1,2,49152]{3,0,2,1:T(2,128)}, /*index=5*/s32[]{:T(128)}, s32[1]{0:T(128)}, s32[]{:T(128)}, s32[]{:T(128)}) while((s32[]{:T(128)}, f32[2,1,60]{2,0,1:T(2,128)S(1)}, s32[8]{0:T(128)S(1)}, ...), condition=%wide.region_9.10_spmd.clone, body=%wide.region_7.9_spmd.clone.sunk | while | flops 6943207 | bytes 3615725 | solution.py:73
  361.9 39.6 %all-reduce = (f32[]{:T(128)}, f32[]{:T(128)}, f32[]{:T(128)}, f32[]{:T(128)}) all-reduce(f32[]{:T(128)} %fusion.53, f32[]{:T(128)} %get-tuple-element.186, f32[]{:T(128)} %fusion.54, f32[]{:T(128)} %get-tuple-element.185), channel_id=1, replica_groups=mesh['cls'=4,'org'=8] {'cls','org'}, use_global_device_ids=true, to_apply=%region_15.16 | all-reduce | flops 4 | bytes 32 | tf_op jit(solution)/shard_map/psum | solution.py:80
  (354 shorter events, 116.3 us)
Async XLA Ops:
  7.2 1.5 copy-start.9
  7.2 167.3 %all-gather.12.cloned.1.call-start = ((), (), s32[]{:S(2)}) async-start(), calls=%async_computation.2 | async-start | bytes 1966080 | tf_op jit(solution)/shard_map/all_gather | solution.py:102
  42.4 1.0 copy-start.1
  42.4 33.8 %collective-permute-start = (f32[2,49152]{1,0:T(2,128)S(1)}, f32[2,49152]{1,0:T(2,128)S(1)}, u32[]{:S(2)}, u32[]{:S(2)}) collective-permute-start(f32[2,49152]{1,0:T(2,128)S(1)} %bitcast.163), channel_id=1, source_target_pairs={{0,1},{1,0},{2,3},{3,2},{4,5},{5,4},{6,7},{7,6},{8,9},{9,8},{10,11... | collective-permute-start | bytes 1179656 | tf_op jit(solution)/shard_map/ppermute | solution.py:18
  75.6 13.6 %copy-start = (s32[2,1,2,49152]{3,0,2,1:T(2,128)}, s32[2,1,2,49152]{3,0,2,1:T(2,128)S(1)}, u32[]{:S(2)}) copy-start(s32[2,1,2,49152]{3,0,2,1:T(2,128)S(1)} %get-tuple-element.489) | copy-start | bytes 2359300
  75.7 3.4 collective-permute-start.3
  76.4 28.1 %copy-start.5 = (f32[2,6144]{1,0:T(2,128)S(1)}, f32[2,6144]{1,0:T(2,128)}, u32[]{:S(2)}) copy-start(f32[2,6144]{1,0:T(2,128)} %param.15) | copy-start | bytes 147460
  76.4 12.6 %collective-permute-start.1 = (f32[2,49152]{1,0:T(2,128)S(1)}, f32[2,49152]{1,0:T(2,128)S(1)}, u32[]{:S(2)}, u32[]{:S(2)}) collective-permute-start(f32[2,49152]{1,0:T(2,128)S(1)} %add.79), channel_id=1, source_target_pairs={{0,2},{1,3},{2,0},{3,1},{4,6},{5,7},{6,4},{7,5},{8,10},{9,11},{10,... | collective-permute-start | bytes 1179656 | tf_op jit(solution)/shard_map/ppermute | solution.py:18
  79.3 58.3 %copy-start.8 = (f32[2]{0:T(128)S(1)}, f32[2]{0:T(128)}, u32[]{:S(2)}) copy-start(f32[2]{0:T(128)} %param.21) | copy-start | bytes 28
  79.3 25.0 %collective-permute-start.4 = (f32[2,49152]{1,0:T(2,128)S(1)}, f32[2,49152]{1,0:T(2,128)S(1)}, u32[]{:S(2)}, u32[]{:S(2)}) collective-permute-start(f32[2,49152]{1,0:T(2,128)S(1)} %add.83), channel_id=1, source_target_pairs={{0,2},{1,3},{2,0},{3,1},{4,6},{5,7},{6,4},{7,5},{8,10},{9,11},{10,... | collective-permute-start | bytes 1179656 | tf_op jit(solution)/shard_map/ppermute | solution.py:18
  89.3 48.9 %collective-permute-start.2 = (f32[2,49152]{1,0:T(2,128)S(1)}, f32[2,49152]{1,0:T(2,128)S(1)}, u32[]{:S(2)}, u32[]{:S(2)}) collective-permute-start(f32[2,49152]{1,0:T(2,128)S(1)} %add.80), channel_id=1, source_target_pairs={{0,4},{1,5},{2,6},{3,7},{4,0},{5,1},{6,2},{7,3},{8,12},{9,13},{10,... | collective-permute-start | bytes 1179656 | tf_op jit(solution)/shard_map/ppermute | solution.py:18
  104.5 33.7 %collective-permute-start.5 = (f32[2,49152]{1,0:T(2,128)S(1)}, f32[2,49152]{1,0:T(2,128)S(1)}, u32[]{:S(2)}, u32[]{:S(2)}) collective-permute-start(f32[2,49152]{1,0:T(2,128)S(1)} %add.84), channel_id=1, source_target_pairs={{0,4},{1,5},{2,6},{3,7},{4,0},{5,1},{6,2},{7,3},{8,12},{9,13},{10,... | collective-permute-start | bytes 1179656 | tf_op jit(solution)/shard_map/ppermute | solution.py:18
  137.5 62.0 %all-gather.10.cloned.1.call-start = ((), (), s32[]{:S(2)}) async-start(), calls=%async_computation.1 | async-start | bytes 1966080 | tf_op jit(solution)/shard_map/all_gather | solution.py:102
  138.2 5.1 %copy-start.7 = (f32[6144]{0:T(1024)S(1)}, f32[6144]{0:T(1024)}, u32[]{:S(2)}) copy-start(f32[6144]{0:T(1024)} %param.18) | copy-start | bytes 73732
  138.2 20.2 %copy-start.6 = (f32[2,6144]{1,0:T(2,128)S(1)}, f32[2,6144]{1,0:T(2,128)}, u32[]{:S(2)}) copy-start(f32[2,6144]{1,0:T(2,128)} %param.17) | copy-start | bytes 147460
  141.9 90.3 %all-gather.14.cloned.1.call-start = ((), (), s32[]{:S(2)}) async-start(), calls=%async_computation.3 | async-start | bytes 1966080 | tf_op jit(solution)/shard_map/all_gather | solution.py:102
  142.7 129.3 %all-gather.8.cloned.1.call-start = ((), (), s32[]{:S(2)}) async-start(), calls=%async_computation | async-start | bytes 3538944 | tf_op jit(solution)/shard_map/all_gather | solution.py:95
  271.9 6.9 %copy-start.2 = (f32[49152]{0:T(1024)S(1)}, f32[49152]{0:T(1024)}, u32[]{:S(2)}) copy-start(f32[49152]{0:T(1024)} %all_gather.25) | copy-start | bytes 589828
  321.9 83.5 %copy-start.3 = (f32[49152]{0:T(1024)S(1)}, f32[49152]{0:T(1024)}, u32[]{:S(2)}) copy-start(f32[49152]{0:T(1024)} %all_gather.25) | copy-start | bytes 589828
  321.9 83.5 %copy-start.4 = (f32[49152,2]{0,1:T(2,128)S(1)}, f32[49152,2]{0,1:T(2,128)}, u32[]{:S(2)}) copy-start(f32[49152,2]{0,1:T(2,128)} %get-tuple-element.184) | copy-start | bytes 1179652
Sparse Core Ops, SparseCore 0:
  137.7 29.1 all-gather.11
  168.6 30.8 all-gather.9
  201.4 30.8 all-gather.13
  233.7 38.1 all-gather.7
